TPU v7x, 128 devices: a whole 4x4x4 slice. The times are simulated.
128 devices in a mesh: grp: 8 (over x, core), dev: 16 (over y, z).
Axes of the slice: x: 4, y: 4, z: 4, core: 2. Of those that a mesh axis runs over, the one named last changes fastest.
Arguments:
- sep_inv: bfloat16 [4096, 4096], P('grp', 'dev'), may hold values from -0.125 to 0.125
- panels: bfloat16 [8, 96, 2048, 128], P('grp', 'dev'), may hold values from -1.1953125 to 1.1953125
- diag_inverse: bfloat16 [8, 96, 768, 128], P('grp', 'dev'), may hold values from -6 to 6
- widths: int32 [8, 32], P('grp'), may hold values from 1 to 6, 96 in all within a row
- ancestors: int32 [8, 32, 16], P('grp'), may hold values from 0 to 31, as said below
Outputs:
- off_diag: bfloat16 [8, 96, 2048, 128], P('grp', 'dev')
- diag_panels: bfloat16 [8, 96, 768, 128], P('grp', 'dev')
Inputs may be any that keep to these rules, and one draw needn't show every extreme that they name: `widths`: each row of a subtree sums to 96. `ancestors`: each supernode's list holds 16 different separator tile numbers in increasing order.
All inputs are finite; a program needn't handle non-finite values.
Results may differ from a plain program's by a relative error of at most 0.0046.
Values may be sent and summed in bfloat16 or wider, within the bound.
A program may use at most 320 MiB of HBM per device.

v0:
```python
import jax
import jax.numpy as jnp
from jax import lax
from jax.sharding import PartitionSpec as P


def extended_2(cells, sides, width):
    for axis, dim in sides:
        count = lax.axis_size(axis)
        ends = count - 1
        head = lax.slice_in_dim(cells, 0, width, axis=dim)
        tail = lax.slice_in_dim(cells, cells.shape[dim] - width, cells.shape[dim], axis=dim)
        cells = jnp.concatenate(
            [
                lax.ppermute(tail, axis, [(i, (i + 1) % count) for i in range(ends)]),
                cells,
                lax.ppermute(head, axis, [((i + 1) % count, i) for i in range(ends)]),
            ],
            axis=dim,
        )
    return cells


def on_device(sep_inv, panels, diag_inverse, widths, ancestors):
    group_count = lax.axis_size("grp")
    device_count = lax.axis_size("dev")
    rows_local = sep_inv.shape[0]
    cols_local = sep_inv.shape[1]
    stacked = lax.all_gather(sep_inv[None], ("grp", "dev"), axis=0, tiled=True)
    whole_sep = stacked.reshape(group_count, device_count, rows_local, cols_local)
    whole_sep = whole_sep.transpose(0, 2, 1, 3).reshape(
        group_count * rows_local, device_count * cols_local
    )
    block = panels.shape[3]
    anc_rows = panels.shape[2]
    anc_tiles = anc_rows // block
    local_units = panels.shape[1]
    max_tiles = diag_inverse.shape[2] // block
    sep_order = whole_sep.shape[0]
    count_blocks = sep_order // block
    row_tiles = whole_sep.reshape(count_blocks, block, sep_order)
    extended = extended_2(panels, (("dev", 1),), max_tiles - 1)
    width_row = widths[0]
    anc_table = ancestors[0]
    supernodes = width_row.shape[0]
    ends = jnp.cumsum(width_row)
    starts = ends - width_row
    position = lax.axis_index("dev") * local_units + jnp.arange(local_units, dtype=jnp.int32)
    owner = jnp.sum((ends[None, :] <= position[:, None]).astype(jnp.int32), axis=1)
    one_hot = (jnp.arange(supernodes, dtype=jnp.int32)[None, :] == owner[:, None]).astype(jnp.int32)
    column = position - jnp.sum(one_hot * starts[None, :], axis=1)
    width_unit = jnp.sum(one_hot * width_row[None, :], axis=1)
    blocks = jnp.sum(one_hot[:, :, None] * anc_table[None, :, :], axis=1)
    tile_ids = jnp.arange(count_blocks, dtype=jnp.int32)

    def per_unit(unit_idx):
        chosen = blocks[unit_idx]
        rows_pick = jnp.take(row_tiles, chosen, axis=0).reshape(anc_rows, sep_order)
        placing = (tile_ids[:, None] == chosen[None, :]).astype(jnp.bfloat16)
        panel_flat = panels[0, unit_idx].reshape(anc_tiles, block * block)
        spread = jnp.dot(placing, panel_flat, preferred_element_type=jnp.float32)
        spread = spread.astype(jnp.bfloat16).reshape(sep_order, block)
        product = jnp.dot(rows_pick, spread, preferred_element_type=jnp.float32)
        result_x = (-product).astype(jnp.bfloat16)
        start_at = unit_idx + max_tiles - 1 - column[unit_idx]
        related = lax.dynamic_slice_in_dim(extended[0], start_at, max_tiles, 0)
        inner = jnp.einsum("jrb,rc->jbc", related, result_x, preferred_element_type=jnp.float32)
        keep = (jnp.arange(max_tiles, dtype=jnp.int32) < width_unit[unit_idx]).astype(jnp.float32)
        diag_block = (
            diag_inverse[0, unit_idx].astype(jnp.float32).reshape(max_tiles, block, block) - inner
        ) * keep[:, None, None]
        return (result_x, diag_block.reshape(max_tiles * block, block).astype(jnp.bfloat16))

    off_diag, diag_panels = lax.map(per_unit, jnp.arange(local_units, dtype=jnp.int32))
    return (off_diag[None], diag_panels[None])


def solution(mesh):
    placed = (
        P("grp", "dev"),
        P("grp", "dev", None, None),
        P("grp", "dev", None, None),
        P("grp", None),
        P("grp", None, None),
    )
    return jax.shard_map(
        on_device,
        mesh=mesh,
        in_specs=placed,
        out_specs=(P("grp", "dev", None, None), P("grp", "dev", None, None)),
        check_vma=False,
    )
```

profile of v0, /device:TPU:1, one launch (start us, length us, event | category | flops | bytes accessed | tf_op | source)
XLA Modules:
  0.0 488.8 jit_solution(15844366094010139155)
XLA Ops:
  7.9 3.2 copy.21
  11.1 3.0 fusion.24
  14.1 5.9 %collective-permute-start = (bf16[1,5,2048,128]{2,3,1,0:T(8,128)(2,1)}, bf16[1,5,2048,128]{2,3,1,0:T(8,128)(2,1)}, u32[]{:S(2)}, u32[]{:S(2)}) collective-permute-start(bf16[1,5,2048,128]{2,3,1,0:T(8,128)(2,1)} %get-tuple-element.293), channel_id=1, source_target_pairs={{0,1},{1,2},{2,3},{3,4},{4,5},{5,6},{6,7},{7,8},{8,9},{9,10},{10,1... | collective-permute-start | bytes 7864328 | tf_op jit(solution)/shard_map/ppermute | solution.py:15
  22.2 54.9 %collective-permute-done = bf16[1,5,2048,128]{2,3,1,0:T(8,128)(2,1)} collective-permute-done((bf16[1,5,2048,128]{2,3,1,0:T(8,128)(2,1)}, bf16[1,5,2048,128]{2,3,1,0:T(8,128)(2,1)}, u32[]{:S(2)}, u32[]{:S(2)}) %collective-permute-start) | collective-permute-done | bytes 2621472 | tf_op jit(solution)/shard_map/ppermute | solution.py:15
  77.1 5.4 %collective-permute-done.1 = bf16[1,5,2048,128]{2,3,1,0:T(8,128)(2,1)} collective-permute-done((bf16[1,5,2048,128]{2,3,1,0:T(8,128)(2,1)}, bf16[1,5,2048,128]{2,3,1,0:T(8,128)(2,1)}, u32[]{:S(2)}, u32[]{:S(2)}) %collective-permute-start.1) | collective-permute-done | bytes 2621472 | tf_op jit(solution)/shard_map/ppermute | solution.py:17
  82.5 6.3 %pad_maximum_fusion = bf16[1,16,2048,128]{2,3,1,0:T(8,128)(2,1)} fusion(bf16[1,5,2048,128]{2,3,1,0:T(8,128)(2,1)} %collective-permute-done.1, bf16[1,6,2048,128]{2,3,1,0:T(8,128)(2,1)S(1)} %copy.21, bf16[1,5,2048,128]{2,3,1,0:T(8,128)(2,1)} %collective-permute-done), kind=kLoop, calls=%fused_computation.29 | loop fusion | flops 8388608 | bytes 16777216 | tf_op jit(solution)/shard_map/concatenate | solution.py:13
  88.8 80.5 %all-gather.3.cloned.1.call-done = bf16[65536,256]{1,0:T(8,128)(2,1)} async-done(((bf16[512,256]{1,0:T(8,128)(2,1)}), bf16[65536,256]{1,0:T(8,128)(2,1)}) %all-gather.3.cloned.1.call-update) | async-done | bytes 33554448 | tf_op jit(solution)/shard_map/all_gather | solution.py:29
  169.3 31.2 %copy.25 = bf16[8,16,512,256]{3,1,2,0:T(8,128)(2,1)} copy(bf16[8,16,512,256]{3,2,1,0:T(8,128)(2,1)} %bitcast.82) | data formatting | bytes 67108864 | tf_op jit(solution)/shard_map/reshape | solution.py:30
  200.5 49.9 %reshape_reshape.3 = bf16[32,128,4096]{2,1,0:T(8,128)(2,1)} reshape(bf16[8,512,16,256]{3,2,1,0:T(8,128)(2,1)} %bitcast.81) | data formatting | bytes 67108864 | tf_op jit(solution)/shard_map/reshape;reshape | solution.py:41
  250.4 231.6 %while.17 = (s32[]{:T(128)}, bf16[6,2048,128]{2,1,0:T(8,128)(2,1)}, bf16[6,768,128]{2,1,0:T(8,128)(2,1)}, s32[6]{0:T(128)S(1)}, s32[6,16]{1,0:T(8,128)S(1)}, /*i...) while((s32[]{:T(128)}, bf16[6,2048,128]{2,1,0:T(8,128)(2,1)}, ...), condition=%wide.region_6.7_spmd.clone, body=%wide.region_5.6_spmd.clone.sunk | while | flops 2576746240 | bytes 96605016 | solution.py:74
  259.7 11.8 %gather_fusion = bf16[16,128,4096]{2,1,0:T(8,128)(2,1)} fusion(bf16[32,128,4096]{2,1,0:T(8,128)(2,1)} %get-tuple-element.407, s32[1024]{0:T(1024)S(1)} %pad_clamp_fusion.2), kind=kCustom, calls=%fused_computation.clone.clone.1 | custom fusion | bytes 33554496 | tf_op jit(solution)/shard_map/while/body/eval_jaxpr/jit(_take)/gather | solution.py:58
  271.4 8.5 %broadcast_select_fusion.2 = bf16[16,128,4096]{2,1,0:T(8,128)(2,1)S(1)} fusion(bf16[16,128,4096]{2,1,0:T(8,128)(2,1)} %gather_fusion, pred[16]{0:T(512)(128)(4,1)S(1)} %get-tuple-element.366), kind=kLoop, calls=%fused_computation.3.clone.1 | loop fusion | flops 8388608 | bytes 33554448 | tf_op jit(solution)/shard_map/while/body/eval_jaxpr/jit(_take)/select_n | solution.py:58
  280.0 5.5 %bitcast_dynamic-update-slice_fusion.4 = (bf16[6,2048,128]{2,1,0:T(8,128)(2,1)}, bf16[2048,128]{1,0:T(8,128)(2,1)S(1)}) fusion(bf16[6,2048,128]{2,1,0:T(8,128)(2,1)} %get-tuple-element.387, s32[]{:T(128)S(6)} %copy.31, bf16[2048,4096]{1,0:T(8,128)(2,1)S(1)} %bitcast.80, bf16[4096,128]{1,0:T(8,128)(2,1)S(1)} %reshape.215), kind=kOutput, calls=%fused_computation.13.clone.1 | convolution fusion | flops 2148007936 | bytes 18874372 | tf_op jit(solution)/shard_map/while/body/eval_jaxpr/dot_general | solution.py:63
  285.4 2.9 fusion.41
  298.3 11.8 %gather_fusion = bf16[16,128,4096]{2,1,0:T(8,128)(2,1)} fusion(bf16[32,128,4096]{2,1,0:T(8,128)(2,1)} %get-tuple-element.407, s32[1024]{0:T(1024)S(1)} %pad_clamp_fusion.2), kind=kCustom, calls=%fused_computation.clone.clone.1 | custom fusion | bytes 33554496 | tf_op jit(solution)/shard_map/while/body/eval_jaxpr/jit(_take)/gather | solution.py:58
  310.0 8.5 %broadcast_select_fusion.2 = bf16[16,128,4096]{2,1,0:T(8,128)(2,1)S(1)} fusion(bf16[16,128,4096]{2,1,0:T(8,128)(2,1)} %gather_fusion, pred[16]{0:T(512)(128)(4,1)S(1)} %get-tuple-element.366), kind=kLoop, calls=%fused_computation.3.clone.1 | loop fusion | flops 8388608 | bytes 33554448 | tf_op jit(solution)/shard_map/while/body/eval_jaxpr/jit(_take)/select_n | solution.py:58
  318.5 5.5 %bitcast_dynamic-update-slice_fusion.4 = (bf16[6,2048,128]{2,1,0:T(8,128)(2,1)}, bf16[2048,128]{1,0:T(8,128)(2,1)S(1)}) fusion(bf16[6,2048,128]{2,1,0:T(8,128)(2,1)} %get-tuple-element.387, s32[]{:T(128)S(6)} %copy.31, bf16[2048,4096]{1,0:T(8,128)(2,1)S(1)} %bitcast.80, bf16[4096,128]{1,0:T(8,128)(2,1)S(1)} %reshape.215), kind=kOutput, calls=%fused_computation.13.clone.1 | convolution fusion | flops 2148007936 | bytes 18874372 | tf_op jit(solution)/shard_map/while/body/eval_jaxpr/dot_general | solution.py:63
  336.8 11.8 %gather_fusion = bf16[16,128,4096]{2,1,0:T(8,128)(2,1)} fusion(bf16[32,128,4096]{2,1,0:T(8,128)(2,1)} %get-tuple-element.407, s32[1024]{0:T(1024)S(1)} %pad_clamp_fusion.2), kind=kCustom, calls=%fused_computation.clone.clone.1 | custom fusion | bytes 33554496 | tf_op jit(solution)/shard_map/while/body/eval_jaxpr/jit(_take)/gather | solution.py:58
  348.6 8.5 %broadcast_select_fusion.2 = bf16[16,128,4096]{2,1,0:T(8,128)(2,1)S(1)} fusion(bf16[16,128,4096]{2,1,0:T(8,128)(2,1)} %gather_fusion, pred[16]{0:T(512)(128)(4,1)S(1)} %get-tuple-element.366), kind=kLoop, calls=%fused_computation.3.clone.1 | loop fusion | flops 8388608 | bytes 33554448 | tf_op jit(solution)/shard_map/while/body/eval_jaxpr/jit(_take)/select_n | solution.py:58
  357.1 5.5 %bitcast_dynamic-update-slice_fusion.4 = (bf16[6,2048,128]{2,1,0:T(8,128)(2,1)}, bf16[2048,128]{1,0:T(8,128)(2,1)S(1)}) fusion(bf16[6,2048,128]{2,1,0:T(8,128)(2,1)} %get-tuple-element.387, s32[]{:T(128)S(6)} %copy.31, bf16[2048,4096]{1,0:T(8,128)(2,1)S(1)} %bitcast.80, bf16[4096,128]{1,0:T(8,128)(2,1)S(1)} %reshape.215), kind=kOutput, calls=%fused_computation.13.clone.1 | convolution fusion | flops 2148007936 | bytes 18874372 | tf_op jit(solution)/shard_map/while/body/eval_jaxpr/dot_general | solution.py:63
  362.6 2.9 fusion.41
  375.4 11.8 %gather_fusion = bf16[16,128,4096]{2,1,0:T(8,128)(2,1)} fusion(bf16[32,128,4096]{2,1,0:T(8,128)(2,1)} %get-tuple-element.407, s32[1024]{0:T(1024)S(1)} %pad_clamp_fusion.2), kind=kCustom, calls=%fused_computation.clone.clone.1 | custom fusion | bytes 33554496 | tf_op jit(solution)/shard_map/while/body/eval_jaxpr/jit(_take)/gather | solution.py:58
  387.2 8.5 %broadcast_select_fusion.2 = bf16[16,128,4096]{2,1,0:T(8,128)(2,1)S(1)} fusion(bf16[16,128,4096]{2,1,0:T(8,128)(2,1)} %gather_fusion, pred[16]{0:T(512)(128)(4,1)S(1)} %get-tuple-element.366), kind=kLoop, calls=%fused_computation.3.clone.1 | loop fusion | flops 8388608 | bytes 33554448 | tf_op jit(solution)/shard_map/while/body/eval_jaxpr/jit(_take)/select_n | solution.py:58
  395.7 5.5 %bitcast_dynamic-update-slice_fusion.4 = (bf16[6,2048,128]{2,1,0:T(8,128)(2,1)}, bf16[2048,128]{1,0:T(8,128)(2,1)S(1)}) fusion(bf16[6,2048,128]{2,1,0:T(8,128)(2,1)} %get-tuple-element.387, s32[]{:T(128)S(6)} %copy.31, bf16[2048,4096]{1,0:T(8,128)(2,1)S(1)} %bitcast.80, bf16[4096,128]{1,0:T(8,128)(2,1)S(1)} %reshape.215), kind=kOutput, calls=%fused_computation.13.clone.1 | convolution fusion | flops 2148007936 | bytes 18874372 | tf_op jit(solution)/shard_map/while/body/eval_jaxpr/dot_general | solution.py:63
  401.2 2.9 fusion.41
  414.0 11.8 %gather_fusion = bf16[16,128,4096]{2,1,0:T(8,128)(2,1)} fusion(bf16[32,128,4096]{2,1,0:T(8,128)(2,1)} %get-tuple-element.407, s32[1024]{0:T(1024)S(1)} %pad_clamp_fusion.2), kind=kCustom, calls=%fused_computation.clone.clone.1 | custom fusion | bytes 33554496 | tf_op jit(solution)/shard_map/while/body/eval_jaxpr/jit(_take)/gather | solution.py:58
  425.8 8.5 %broadcast_select_fusion.2 = bf16[16,128,4096]{2,1,0:T(8,128)(2,1)S(1)} fusion(bf16[16,128,4096]{2,1,0:T(8,128)(2,1)} %gather_fusion, pred[16]{0:T(512)(128)(4,1)S(1)} %get-tuple-element.366), kind=kLoop, calls=%fused_computation.3.clone.1 | loop fusion | flops 8388608 | bytes 33554448 | tf_op jit(solution)/shard_map/while/body/eval_jaxpr/jit(_take)/select_n | solution.py:58
  434.3 5.5 %bitcast_dynamic-update-slice_fusion.4 = (bf16[6,2048,128]{2,1,0:T(8,128)(2,1)}, bf16[2048,128]{1,0:T(8,128)(2,1)S(1)}) fusion(bf16[6,2048,128]{2,1,0:T(8,128)(2,1)} %get-tuple-element.387, s32[]{:T(128)S(6)} %copy.31, bf16[2048,4096]{1,0:T(8,128)(2,1)S(1)} %bitcast.80, bf16[4096,128]{1,0:T(8,128)(2,1)S(1)} %reshape.215), kind=kOutput, calls=%fused_computation.13.clone.1 | convolution fusion | flops 2148007936 | bytes 18874372 | tf_op jit(solution)/shard_map/while/body/eval_jaxpr/dot_general | solution.py:63
  439.8 2.9 fusion.41
  452.7 11.8 %gather_fusion = bf16[16,128,4096]{2,1,0:T(8,128)(2,1)} fusion(bf16[32,128,4096]{2,1,0:T(8,128)(2,1)} %get-tuple-element.407, s32[1024]{0:T(1024)S(1)} %pad_clamp_fusion.2), kind=kCustom, calls=%fused_computation.clone.clone.1 | custom fusion | bytes 33554496 | tf_op jit(solution)/shard_map/while/body/eval_jaxpr/jit(_take)/gather | solution.py:58
  464.4 8.5 %broadcast_select_fusion.2 = bf16[16,128,4096]{2,1,0:T(8,128)(2,1)S(1)} fusion(bf16[16,128,4096]{2,1,0:T(8,128)(2,1)} %gather_fusion, pred[16]{0:T(512)(128)(4,1)S(1)} %get-tuple-element.366), kind=kLoop, calls=%fused_computation.3.clone.1 | loop fusion | flops 8388608 | bytes 33554448 | tf_op jit(solution)/shard_map/while/body/eval_jaxpr/jit(_take)/select_n | solution.py:58
  472.9 5.5 %bitcast_dynamic-update-slice_fusion.4 = (bf16[6,2048,128]{2,1,0:T(8,128)(2,1)}, bf16[2048,128]{1,0:T(8,128)(2,1)S(1)}) fusion(bf16[6,2048,128]{2,1,0:T(8,128)(2,1)} %get-tuple-element.387, s32[]{:T(128)S(6)} %copy.31, bf16[2048,4096]{1,0:T(8,128)(2,1)S(1)} %bitcast.80, bf16[4096,128]{1,0:T(8,128)(2,1)S(1)} %reshape.215), kind=kOutput, calls=%fused_computation.13.clone.1 | convolution fusion | flops 2148007936 | bytes 18874372 | tf_op jit(solution)/shard_map/while/body/eval_jaxpr/dot_general | solution.py:63
  (100 shorter events, 47.9 us)
Async XLA Ops:
  7.2 162.2 %all-gather.3.cloned.1.call-start = ((), (), s32[]{:S(2)}) async-start(), calls=%async_computation | async-start | bytes 33816576 | tf_op jit(solution)/shard_map/all_gather | solution.py:29
  11.1 10.2 %copy-start.1 = (s32[1,32]{1,0:T(1,128)S(1)}, s32[1,32]{1,0:T(1,128)}, u32[]{:S(2)}) copy-start(s32[1,32]{1,0:T(1,128)} %param.10) | copy-start | bytes 388
  11.1 10.7 %copy-start = (s32[1,32,16]{1,2,0:T(8,128)S(1)}, s32[1,32,16]{1,2,0:T(8,128)}, u32[]{:S(2)}) copy-start(s32[1,32,16]{1,2,0:T(8,128)} %param.11) | copy-start | bytes 6148
  14.1 63.0 %collective-permute-start = (bf16[1,5,2048,128]{2,3,1,0:T(8,128)(2,1)}, bf16[1,5,2048,128]{2,3,1,0:T(8,128)(2,1)}, u32[]{:S(2)}, u32[]{:S(2)}) collective-permute-start(bf16[1,5,2048,128]{2,3,1,0:T(8,128)(2,1)} %get-tuple-element.293), channel_id=1, source_target_pairs={{0,1},{1,2},{2,3},{3,4},{4,5},{5,6},{6,7},{7,8},{8,9},{9,10},{10,1... | collective-permute-start | bytes 7864328 | tf_op jit(solution)/shard_map/ppermute | solution.py:15
  20.0 62.5 %collective-permute-start.1 = (bf16[1,5,2048,128]{2,3,1,0:T(8,128)(2,1)}, bf16[1,5,2048,128]{2,3,1,0:T(8,128)(2,1)}, u32[]{:S(2)}, u32[]{:S(2)}) collective-permute-start(bf16[1,5,2048,128]{2,3,1,0:T(8,128)(2,1)} %get-tuple-element.294), channel_id=1, source_target_pairs={{1,0},{2,1},{3,2},{4,3},{5,4},{6,5},{7,6},{8,7},{9,8},{10,9},{11,1... | collective-permute-start | bytes 7864328 | tf_op jit(solution)/shard_map/ppermute | solution.py:17
Sparse Core Ops, SparseCore 0:
  11.1 158.1 all-gather.2
where the time goes:
time: 492 us; the launch traced here: 489 us
  local copies, waits for them, and re-layouts  191 us (39%)
  waiting for transfers between devices  141 us (29%)
  other arithmetic  62.4 us (13%)
  matrix products  52.4 us (11%)
  loops' own time  20.7 us (4%)
  between operations  14.1 us (3%)
  starting transfers between devices  7.21 us (1%)
    all_gather x1, waiting for transfers between devices, on_device(): stacked = lax.all_gather(sep_inv[None], ('grp', 'dev'), axis=0, tiled=True)  80.5 us
    gather x6, local copies, waits for them, and re-layouts, per_unit(): rows_pick = jnp.take(row_tiles, chosen, axis=0).reshape(anc_rows, sep_order)  70.6 us
    ppermute x1, waiting for transfers between devices, extended_2(): lax.ppermute(tail, axis, [(i, (i + 1) % count) for i in range(ends)])  54.9 us
    select_n x12, other arithmetic, per_unit(): rows_pick = jnp.take(row_tiles, chosen, axis=0).reshape(anc_rows, sep_order)  51.1 us
    another operation x1, local copies, waits for them, and re-layouts, on_device(): row_tiles = whole_sep.reshape(count_blocks, block, sep_order)  49.9 us
    dot_general x6, matrix products, per_unit(): product = jnp.dot(rows_pick, spread, preferred_element_type=jnp.float32)  32.8 us
    reshape x1, local copies, waits for them, and re-layouts, on_device(): stacked.reshape(group_count, device_count, rows_local, cols_local)  31.2 us
    another operation x1, loops' own time, on_device(): lax.map(per_unit, jnp.arange(local_units, dtype=jnp.int32))  20.7 us
  transfers between devices with their start and end apart: 3, of which 3 were waited for; matrix products, arithmetic and copies ran while one was open for 3% of the time, Pallas kernels for 0%

commit v1 on v0

--- a/solution.py
+++ b/solution.py
@@ -26,7 +26,12 @@
     device_count = lax.axis_size("dev")
     rows_local = sep_inv.shape[0]
     cols_local = sep_inv.shape[1]
-    stacked = lax.all_gather(sep_inv[None], ("grp", "dev"), axis=0, tiled=True)
+    stacked = jnp.concatenate(
+        lax.all_to_all(
+            jnp.stack([sep_inv[None]] * lax.axis_size(("grp", "dev"))), ("grp", "dev"), 0, 0
+        ),
+        axis=0,
+    )
     whole_sep = stacked.reshape(group_count, device_count, rows_local, cols_local)
     whole_sep = whole_sep.transpose(0, 2, 1, 3).reshape(
         group_count * rows_local, device_count * cols_local

time: 492 us -> 927 us (1.88)
  the two profiles are of different devices: /device:TPU:1 before, /device:TPU:14 now
where the time goes in v1:
time: 927 us; the launch traced here: 924 us
  waiting for transfers between devices  514 us (55%)
  local copies, waits for them, and re-layouts  202 us (22%)
  other arithmetic  96 us (10%)
  matrix products  74 us (8%)
  loops' own time  19.2 us (2%)
  starting transfers between devices  18 us (2%)
    ppermute x1, waiting for transfers between devices, extended_2(): lax.ppermute(head, axis, [((i + 1) % count, i) for i in range(ends)])  500 us
    select_n x12, other arithmetic, per_unit(): rows_pick = jnp.take(row_tiles, chosen, axis=0).reshape(anc_rows, sep_order)  85 us
    gather x6, local copies, waits for them, and re-layouts, per_unit(): rows_pick = jnp.take(row_tiles, chosen, axis=0).reshape(anc_rows, sep_order)  70.6 us
    dot_general x6, matrix products, per_unit(): product = jnp.dot(rows_pick, spread, preferred_element_type=jnp.float32)  54.3 us
    another operation x1, local copies, waits for them, and re-layouts, on_device(): row_tiles = whole_sep.reshape(count_blocks, block, sep_order)  49.9 us
    transpose x1, local copies, waits for them, and re-layouts, on_device(): whole_sep.transpose(0, 2, 1, 3)  31.2 us
    another operation x1, loops' own time, on_device(): lax.map(per_unit, jnp.arange(local_units, dtype=jnp.int32))  19.2 us
  transfers between devices with their start and end apart: 3, of which 2 were waited for; matrix products, arithmetic and copies ran while one was open for 1% of the time, Pallas kernels for 0%

profile of v1, /device:TPU:14, one launch (start us, length us, event | category | flops | bytes accessed | tf_op | source)
XLA Modules:
  0.0 924.3 jit_solution(18005154484900116020)
XLA Ops:
  0.6 11.7 %stack.3 = bf16[128,1,512,256]{3,2,1,0:T(8,128)(2,1)} broadcast(bf16[512,256]{1,0:T(8,128)(2,1)} %param.7), dimensions={2,3} | broadcast | bytes 33816576 | tf_op jit(solution)/shard_map/stack | solution.py:31
  12.3 10.8 %all-to-all-start = ((bf16[128,1,512,256]{3,2,1,0:T(8,128)(2,1)}), bf16[128,1,512,256]{3,2,1,0:T(8,128)(2,1)}, u32[]{:S(2)}, u32[]{:S(2)}) async-start(bf16[128,1,512,256]{3,2,1,0:T(8,128)(2,1)} %stack.3), calls=%async_computation | async-start | bytes 67108864 | tf_op jit(solution)/shard_map/all_to_all | solution.py:30
  23.1 3.2 copy.31
  26.4 3.0 fusion.24
  29.4 5.3 collective-permute-start.1
  37.5 499.7 %collective-permute-done.1 = bf16[1,5,2048,128]{2,3,1,0:T(8,128)(2,1)} collective-permute-done((bf16[1,5,2048,128]{2,3,1,0:T(8,128)(2,1)}, bf16[1,5,2048,128]{2,3,1,0:T(8,128)(2,1)}, u32[]{:S(2)}, u32[]{:S(2)}) %collective-permute-start.1) | collective-permute-done | bytes 2621472 | tf_op jit(solution)/shard_map/ppermute | solution.py:17
  537.2 14.7 %collective-permute-done = bf16[1,5,2048,128]{2,3,1,0:T(8,128)(2,1)} collective-permute-done((bf16[1,5,2048,128]{2,3,1,0:T(8,128)(2,1)}, bf16[1,5,2048,128]{2,3,1,0:T(8,128)(2,1)}, u32[]{:S(2)}, u32[]{:S(2)}) %collective-permute-start) | collective-permute-done | bytes 2621472 | tf_op jit(solution)/shard_map/ppermute | solution.py:15
  551.9 6.3 pad_maximum_fusion
  558.3 31.2 %copy.30 = bf16[8,512,16,256]{3,2,1,0:T(8,128)(2,1)} copy(bf16[8,512,16,256]{3,1,2,0:T(8,128)(2,1)} %bitcast.3) | data formatting | bytes 67108864 | tf_op jit(solution)/shard_map/transpose | solution.py:36
  589.4 49.9 %reshape_reshape.7 = bf16[32,128,4096]{2,1,0:T(8,128)(2,1)} reshape(bf16[8,512,16,256]{3,2,1,0:T(8,128)(2,1)} %copy.30) | data formatting | bytes 67108864 | tf_op jit(solution)/shard_map/reshape;reshape | solution.py:46
  639.3 285.0 %while.17 = (s32[]{:T(128)}, bf16[6,2048,128]{2,1,0:T(8,128)(2,1)}, bf16[6,768,128]{2,1,0:T(8,128)(2,1)}, s32[6]{0:T(128)S(1)}, s32[6,16]{1,0:T(8,128)S(1)}, /*i...) while((s32[]{:T(128)}, bf16[6,2048,128]{2,1,0:T(8,128)(2,1)}, ...), condition=%wide.region_6.7_spmd.clone, body=%wide.region_5.6_spmd.clone.sunk | while | flops 2576746240 | bytes 96605016 | solution.py:79
  641.9 11.8 %gather_fusion = bf16[16,128,4096]{2,1,0:T(8,128)(2,1)} fusion(bf16[32,128,4096]{2,1,0:T(8,128)(2,1)} %get-tuple-element.407, s32[1024]{0:T(1024)S(1)} %pad_clamp_fusion.2), kind=kCustom, calls=%fused_computation.clone.clone.1 | custom fusion | bytes 33554496 | tf_op jit(solution)/shard_map/while/body/eval_jaxpr/jit(_take)/gather | solution.py:63
  653.7 14.2 %broadcast_select_fusion.2 = bf16[16,128,4096]{2,1,0:T(8,128)(2,1)} fusion(bf16[16,128,4096]{2,1,0:T(8,128)(2,1)} %gather_fusion, pred[16]{0:T(512)(128)(4,1)S(1)} %get-tuple-element.366), kind=kLoop, calls=%fused_computation.3.clone.1 | loop fusion | flops 8388608 | bytes 33554448 | tf_op jit(solution)/shard_map/while/body/eval_jaxpr/jit(_take)/select_n | solution.py:63
  670.1 9.1 bitcast_dynamic-update-slice_fusion.4
  689.4 11.8 %gather_fusion = bf16[16,128,4096]{2,1,0:T(8,128)(2,1)} fusion(bf16[32,128,4096]{2,1,0:T(8,128)(2,1)} %get-tuple-element.407, s32[1024]{0:T(1024)S(1)} %pad_clamp_fusion.2), kind=kCustom, calls=%fused_computation.clone.clone.1 | custom fusion | bytes 33554496 | tf_op jit(solution)/shard_map/while/body/eval_jaxpr/jit(_take)/gather | solution.py:63
  701.1 14.2 %broadcast_select_fusion.2 = bf16[16,128,4096]{2,1,0:T(8,128)(2,1)} fusion(bf16[16,128,4096]{2,1,0:T(8,128)(2,1)} %gather_fusion, pred[16]{0:T(512)(128)(4,1)S(1)} %get-tuple-element.366), kind=kLoop, calls=%fused_computation.3.clone.1 | loop fusion | flops 8388608 | bytes 33554448 | tf_op jit(solution)/shard_map/while/body/eval_jaxpr/jit(_take)/select_n | solution.py:63
  717.6 9.1 bitcast_dynamic-update-slice_fusion.4
  730.8 2.9 fusion.41
  736.9 11.8 %gather_fusion = bf16[16,128,4096]{2,1,0:T(8,128)(2,1)} fusion(bf16[32,128,4096]{2,1,0:T(8,128)(2,1)} %get-tuple-element.407, s32[1024]{0:T(1024)S(1)} %pad_clamp_fusion.2), kind=kCustom, calls=%fused_computation.clone.clone.1 | custom fusion | bytes 33554496 | tf_op jit(solution)/shard_map/while/body/eval_jaxpr/jit(_take)/gather | solution.py:63
  748.7 14.2 %broadcast_select_fusion.2 = bf16[16,128,4096]{2,1,0:T(8,128)(2,1)} fusion(bf16[16,128,4096]{2,1,0:T(8,128)(2,1)} %gather_fusion, pred[16]{0:T(512)(128)(4,1)S(1)} %get-tuple-element.366), kind=kLoop, calls=%fused_computation.3.clone.1 | loop fusion | flops 8388608 | bytes 33554448 | tf_op jit(solution)/shard_map/while/body/eval_jaxpr/jit(_take)/select_n | solution.py:63
  765.1 9.1 bitcast_dynamic-update-slice_fusion.4
  784.4 11.8 %gather_fusion = bf16[16,128,4096]{2,1,0:T(8,128)(2,1)} fusion(bf16[32,128,4096]{2,1,0:T(8,128)(2,1)} %get-tuple-element.407, s32[1024]{0:T(1024)S(1)} %pad_clamp_fusion.2), kind=kCustom, calls=%fused_computation.clone.clone.1 | custom fusion | bytes 33554496 | tf_op jit(solution)/shard_map/while/body/eval_jaxpr/jit(_take)/gather | solution.py:63
  796.1 14.2 %broadcast_select_fusion.2 = bf16[16,128,4096]{2,1,0:T(8,128)(2,1)} fusion(bf16[16,128,4096]{2,1,0:T(8,128)(2,1)} %gather_fusion, pred[16]{0:T(512)(128)(4,1)S(1)} %get-tuple-element.366), kind=kLoop, calls=%fused_computation.3.clone.1 | loop fusion | flops 8388608 | bytes 33554448 | tf_op jit(solution)/shard_map/while/body/eval_jaxpr/jit(_take)/select_n | solution.py:63
  812.6 9.1 bitcast_dynamic-update-slice_fusion.4
  825.8 2.9 fusion.41
  831.9 11.8 %gather_fusion = bf16[16,128,4096]{2,1,0:T(8,128)(2,1)} fusion(bf16[32,128,4096]{2,1,0:T(8,128)(2,1)} %get-tuple-element.407, s32[1024]{0:T(1024)S(1)} %pad_clamp_fusion.2), kind=kCustom, calls=%fused_computation.clone.clone.1 | custom fusion | bytes 33554496 | tf_op jit(solution)/shard_map/while/body/eval_jaxpr/jit(_take)/gather | solution.py:63
  843.7 14.2 %broadcast_select_fusion.2 = bf16[16,128,4096]{2,1,0:T(8,128)(2,1)} fusion(bf16[16,128,4096]{2,1,0:T(8,128)(2,1)} %gather_fusion, pred[16]{0:T(512)(128)(4,1)S(1)} %get-tuple-element.366), kind=kLoop, calls=%fused_computation.3.clone.1 | loop fusion | flops 8388608 | bytes 33554448 | tf_op jit(solution)/shard_map/while/body/eval_jaxpr/jit(_take)/select_n | solution.py:63
  860.1 9.1 bitcast_dynamic-update-slice_fusion.4
  879.4 11.8 %gather_fusion = bf16[16,128,4096]{2,1,0:T(8,128)(2,1)} fusion(bf16[32,128,4096]{2,1,0:T(8,128)(2,1)} %get-tuple-element.407, s32[1024]{0:T(1024)S(1)} %pad_clamp_fusion.2), kind=kCustom, calls=%fused_computation.clone.clone.1 | custom fusion | bytes 33554496 | tf_op jit(solution)/shard_map/while/body/eval_jaxpr/jit(_take)/gather | solution.py:63
  891.1 14.2 %broadcast_select_fusion.2 = bf16[16,128,4096]{2,1,0:T(8,128)(2,1)} fusion(bf16[16,128,4096]{2,1,0:T(8,128)(2,1)} %gather_fusion, pred[16]{0:T(512)(128)(4,1)S(1)} %get-tuple-element.366), kind=kLoop, calls=%fused_computation.3.clone.1 | loop fusion | flops 8388608 | bytes 33554448 | tf_op jit(solution)/shard_map/while/body/eval_jaxpr/jit(_take)/select_n | solution.py:63
  907.6 9.1 bitcast_dynamic-update-slice_fusion.4
  920.8 2.9 fusion.41
  (100 shorter events, 50.1 us)
Async XLA Ops:
  12.3 545.9 %all-to-all-start = ((bf16[128,1,512,256]{3,2,1,0:T(8,128)(2,1)}), bf16[128,1,512,256]{3,2,1,0:T(8,128)(2,1)}, u32[]{:S(2)}, u32[]{:S(2)}) async-start(bf16[128,1,512,256]{3,2,1,0:T(8,128)(2,1)} %stack.3), calls=%async_computation | async-start | bytes 67108864 | tf_op jit(solution)/shard_map/all_to_all | solution.py:30
  26.4 10.2 %copy-start.1 = (s32[1,32]{1,0:T(1,128)S(1)}, s32[1,32]{1,0:T(1,128)}, u32[]{:S(2)}) copy-start(s32[1,32]{1,0:T(1,128)} %param.10) | copy-start | bytes 388
  26.4 10.8 %copy-start = (s32[1,32,16]{1,2,0:T(8,128)S(1)}, s32[1,32,16]{1,2,0:T(8,128)}, u32[]{:S(2)}) copy-start(s32[1,32,16]{1,2,0:T(8,128)} %param.11) | copy-start | bytes 6148
  29.4 507.8 %collective-permute-start.1 = (bf16[1,5,2048,128]{2,3,1,0:T(8,128)(2,1)}, bf16[1,5,2048,128]{2,3,1,0:T(8,128)(2,1)}, u32[]{:S(2)}, u32[]{:S(2)}) collective-permute-start(bf16[1,5,2048,128]{2,3,1,0:T(8,128)(2,1)} %get-tuple-element.294), channel_id=1, source_target_pairs={{1,0},{2,1},{3,2},{4,3},{5,4},{6,5},{7,6},{8,7},{9,8},{10,9},{11,1... | collective-permute-start | bytes 7864328 | tf_op jit(solution)/shard_map/ppermute | solution.py:17
  34.6 517.3 %collective-permute-start = (bf16[1,5,2048,128]{2,3,1,0:T(8,128)(2,1)}, bf16[1,5,2048,128]{2,3,1,0:T(8,128)(2,1)}, u32[]{:S(2)}, u32[]{:S(2)}) collective-permute-start(bf16[1,5,2048,128]{2,3,1,0:T(8,128)(2,1)} %get-tuple-element.293), channel_id=1, source_target_pairs={{0,1},{1,2},{2,3},{3,4},{4,5},{5,6},{6,7},{7,8},{8,9},{9,10},{10,1... | collective-permute-start | bytes 7864328 | tf_op jit(solution)/shard_map/ppermute | solution.py:15
